TPU v7x, 32 devices: a whole 2x2x4 slice. The times are simulated.
32 devices in a mesh: dp: 8 (over y, x, core), fsdp: 4 (over z).
Axes of the slice: x: 2, y: 2, z: 4, core: 2. Of those that a mesh axis runs over, the one named last changes fastest.
Arguments:
- tokens: bfloat16 [19200, 1024], P(('dp', 'fsdp')), may hold values from -6 to 6
- cotangent: bfloat16 [19200, 1024], P(('dp', 'fsdp')), may hold values from -6 to 6
- crop_group: int32 [8], P('dp'), may hold values from 0 to 1, as said below
- group_tokens: int32 [2], replicated, may hold values from 1000 to 7999
- qkv_weight: float32 [1024, 3072], P('fsdp'), may hold values from -0.1875 to 0.1875
- query_bias: float32 [1024], P('fsdp'), may hold values from -2 to 2
- value_bias: float32 [1024], P('fsdp'), may hold values from -2 to 2
- out_weight: float32 [1024, 1024], P('fsdp'), may hold values from -0.375 to 0.375
- out_bias: float32 [1024], P('fsdp'), may hold values from -2 to 2
- attn_gain: float32 [1024], P('fsdp'), may hold values from 0.5 to 1.5
- attn_shift: float32 [1024], P('fsdp'), may hold values from -2 to 2
- mlp_gain: float32 [1024], P('fsdp'), may hold values from 0.5 to 1.5
- mlp_shift: float32 [1024], P('fsdp'), may hold values from -2 to 2
- up_weight: float32 [1024, 4096], P('fsdp'), may hold values from -0.1875 to 0.1875
- up_bias: float32 [4096], P('fsdp'), may hold values from -2 to 2
- down_weight: float32 [4096, 1024], P('fsdp'), may hold values from -0.09375 to 0.09375
- down_bias: float32 [1024], P('fsdp'), may hold values from -2 to 2
Outputs:
- mixed_out: bfloat16 [19200, 1024], P(('dp', 'fsdp'))
- grad_tokens: bfloat16 [19200, 1024], P(('dp', 'fsdp'))
- grad_qkv_weight: float32 [1024, 3072], P('fsdp')
- grad_query_bias: float32 [1024], P('fsdp')
- grad_value_bias: float32 [1024], P('fsdp')
- grad_out_weight: float32 [1024, 1024], P('fsdp')
- grad_out_bias: float32 [1024], P('fsdp')
- grad_attn_gain: float32 [1024], P('fsdp')
- grad_attn_shift: float32 [1024], P('fsdp')
- grad_mlp_gain: float32 [1024], P('fsdp')
- grad_mlp_shift: float32 [1024], P('fsdp')
- grad_up_weight: float32 [1024, 4096], P('fsdp')
- grad_up_bias: float32 [4096], P('fsdp')
- grad_down_weight: float32 [4096, 1024], P('fsdp')
- grad_down_bias: float32 [1024], P('fsdp')
Inputs may be any that keep to these rules, and one draw needn't show every extreme that they name: `crop_group`: exactly 5 entries are 1 and the others 0.
All inputs are finite; a program needn't handle non-finite values.
Results may differ from a plain program's by a relative error of at most 0.02.
Values may be sent and summed in bfloat16 or wider, within the bound.
A program may use at most 192 MiB of HBM per device.

v0:
```python
import jax
import jax.numpy as jnp
from jax import lax
from jax.sharding import PartitionSpec as P

D = 1024
HEADS = 16
HEAD_DIM = 64
GLEN = 50
LLEN = 10


EPSILON = 1e-06
ROOT_HALF = 0.7071067811865476
INV_ROOT_TAU = 0.3989422804014327


def normalize(values):
    middle = jnp.mean(values, axis=-1, keepdims=True)
    centered = values - middle
    inverse = lax.rsqrt(jnp.mean(centered * centered, axis=-1, keepdims=True) + EPSILON)
    return (centered * inverse, inverse)


def norm_back(grad_out, gain, scaled, inverse):
    grad_scaled = grad_out * gain
    return inverse * (
        grad_scaled
        - jnp.mean(grad_scaled, axis=-1, keepdims=True)
        - scaled * jnp.mean(grad_scaled * scaled, axis=-1, keepdims=True)
    )


def by_crops(values, crop):
    return values.reshape(values.shape[0] // crop, crop, HEADS, HEAD_DIM)


def crop_scores(queries, key_rows):
    factor = HEAD_DIM ** (-0.5)
    return (
        jnp.einsum("cqhd,ckhd->chqk", queries, key_rows, preferred_element_type=jnp.float32)
        * factor
    )


def attend_crops(queries, key_rows, value_rows, crop):
    length = queries.shape[0]
    crop_q, crop_k, crop_v = (
        by_crops(queries, crop),
        by_crops(key_rows, crop),
        by_crops(value_rows, crop),
    )
    scores = crop_scores(crop_q, crop_k)
    highest = jnp.max(scores, axis=-1, keepdims=True)
    exponent = jnp.exp(scores - highest)
    summed = jnp.sum(exponent, axis=-1, keepdims=True)
    attention = (exponent / summed).astype(jnp.bfloat16)
    context = jnp.einsum("chqk,ckhd->cqhd", attention, crop_v, preferred_element_type=jnp.float32)
    logsum = (highest + jnp.log(summed))[..., 0]
    return (
        context.reshape(length, HEADS * HEAD_DIM),
        jnp.transpose(logsum, (0, 2, 1)).reshape(length, HEADS),
    )


def attend_crops_back(queries, key_rows, value_rows, logsum, grad_context, crop):
    length = queries.shape[0]
    factor = HEAD_DIM ** (-0.5)
    crop_q, crop_k, crop_v = (
        by_crops(queries, crop),
        by_crops(key_rows, crop),
        by_crops(value_rows, crop),
    )
    crop_g = by_crops(grad_context, crop)
    crop_l = jnp.transpose(logsum.reshape(length // crop, crop, HEADS), (0, 2, 1))
    scores = crop_scores(crop_q, crop_k)
    probs = jnp.exp(scores - crop_l[..., None])
    probs_low = probs.astype(jnp.bfloat16)
    grad_values = jnp.einsum(
        "chqk,cqhd->ckhd", probs_low, crop_g, preferred_element_type=jnp.float32
    )
    grad_probs = jnp.einsum("cqhd,ckhd->chqk", crop_g, crop_v, preferred_element_type=jnp.float32)
    delta = jnp.sum(probs * grad_probs, axis=-1, keepdims=True)
    grad_scores = (probs * (grad_probs - delta)).astype(jnp.bfloat16)
    grad_queries = (
        jnp.einsum("chqk,ckhd->cqhd", grad_scores, crop_k, preferred_element_type=jnp.float32)
        * factor
    )
    grad_keys = (
        jnp.einsum("chqk,cqhd->ckhd", grad_scores, crop_q, preferred_element_type=jnp.float32)
        * factor
    )
    width = HEADS * HEAD_DIM
    return jnp.concatenate(
        [
            grad_queries.reshape(length, width),
            grad_keys.reshape(length, width),
            grad_values.reshape(length, width),
        ],
        axis=1,
    ).astype(jnp.bfloat16)


def column_sums(values):
    return jnp.sum(values.astype(jnp.float32), axis=0)


def local(
    tokens,
    cotangent,
    crop_group,
    group_tokens,
    qkv_weight,
    query_bias,
    value_bias,
    out_weight,
    out_bias,
    attn_gain,
    attn_shift,
    mlp_gain,
    mlp_shift,
    up_weight,
    up_bias,
    down_weight,
    down_bias,
):
    gathered = (
        lax.all_gather(qkv_weight.astype(jnp.bfloat16), "fsdp", axis=0, tiled=True),
        lax.all_gather(query_bias.astype(jnp.bfloat16), "fsdp", axis=0, tiled=True),
        lax.all_gather(value_bias.astype(jnp.bfloat16), "fsdp", axis=0, tiled=True),
        lax.all_gather(out_weight.astype(jnp.bfloat16), "fsdp", axis=0, tiled=True),
        lax.all_gather(out_bias.astype(jnp.bfloat16), "fsdp", axis=0, tiled=True),
        lax.all_gather(attn_gain.astype(jnp.bfloat16), "fsdp", axis=0, tiled=True),
        lax.all_gather(attn_shift.astype(jnp.bfloat16), "fsdp", axis=0, tiled=True),
        lax.all_gather(mlp_gain.astype(jnp.bfloat16), "fsdp", axis=0, tiled=True),
        lax.all_gather(mlp_shift.astype(jnp.bfloat16), "fsdp", axis=0, tiled=True),
        lax.all_gather(up_weight.astype(jnp.bfloat16), "fsdp", axis=0, tiled=True),
        lax.all_gather(up_bias.astype(jnp.bfloat16), "fsdp", axis=0, tiled=True),
        lax.all_gather(down_weight.astype(jnp.bfloat16), "fsdp", axis=0, tiled=True),
        lax.all_gather(down_bias.astype(jnp.bfloat16), "fsdp", axis=0, tiled=True),
    )
    (
        qkv_low,
        query_add,
        value_add,
        out_low,
        out_add,
        gain_one,
        shift_one,
        gain_two,
        shift_two,
        up_low,
        up_add,
        down_low,
        down_add,
    ) = gathered
    query_add = query_add.astype(jnp.float32)
    value_add = value_add.astype(jnp.float32)
    out_add = out_add.astype(jnp.float32)
    gain_one = gain_one.astype(jnp.float32)
    shift_one = shift_one.astype(jnp.float32)
    gain_two = gain_two.astype(jnp.float32)
    shift_two = shift_two.astype(jnp.float32)
    up_add = up_add.astype(jnp.float32)
    down_add = down_add.astype(jnp.float32)
    is_global = crop_group[0] == 1
    totals = (group_tokens[0] + group_tokens[1]).astype(jnp.float32)
    loss_share = jnp.where(is_global, group_tokens[1], group_tokens[0]).astype(jnp.float32) / totals
    inputs = tokens.astype(jnp.float32)
    scaled_one, inverse_one = normalize(inputs)
    normed_one = (scaled_one * gain_one + shift_one).astype(jnp.bfloat16)
    projected = jnp.dot(normed_one, qkv_low, preferred_element_type=jnp.float32)
    projected = projected + jnp.concatenate([query_add, jnp.zeros_like(query_add), value_add])
    projected_low = projected.astype(jnp.bfloat16)
    queries = projected_low[:, :D]
    key_rows = projected_low[:, D : 2 * D]
    value_rows = projected_low[:, 2 * D :]
    context, logsum = lax.cond(
        is_global,
        lambda parts: attend_crops(parts[0], parts[1], parts[2], GLEN),
        lambda parts: attend_crops(parts[0], parts[1], parts[2], LLEN),
        (queries, key_rows, value_rows),
    )
    context_low = context.astype(jnp.bfloat16)
    middle = inputs + (jnp.dot(context_low, out_low, preferred_element_type=jnp.float32) + out_add)
    scaled_two, inverse_two = normalize(middle)
    normed_two = (scaled_two * gain_two + shift_two).astype(jnp.bfloat16)
    preacts = jnp.dot(normed_two, up_low, preferred_element_type=jnp.float32) + up_add
    error_part = 1.0 + jax.scipy.special.erf(preacts * ROOT_HALF)
    activated = (0.5 * preacts * error_part).astype(jnp.bfloat16)
    mixed_out = (
        middle + (jnp.dot(activated, down_low, preferred_element_type=jnp.float32) + down_add)
    ).astype(jnp.bfloat16)
    qkv_back, out_back, up_back, down_back, gain_one_back, gain_two_back = (
        lax.all_gather(qkv_weight.astype(jnp.bfloat16), "fsdp", axis=0, tiled=True),
        lax.all_gather(out_weight.astype(jnp.bfloat16), "fsdp", axis=0, tiled=True),
        lax.all_gather(up_weight.astype(jnp.bfloat16), "fsdp", axis=0, tiled=True),
        lax.all_gather(down_weight.astype(jnp.bfloat16), "fsdp", axis=0, tiled=True),
        lax.all_gather(attn_gain.astype(jnp.bfloat16), "fsdp", axis=0, tiled=True),
        lax.all_gather(mlp_gain.astype(jnp.bfloat16), "fsdp", axis=0, tiled=True),
    )
    gain_one_back = gain_one_back.astype(jnp.float32)
    gain_two_back = gain_two_back.astype(jnp.float32)
    upstream = cotangent.astype(jnp.float32) * loss_share
    upstream_low = upstream.astype(jnp.bfloat16)
    grad_down_weight = jnp.dot(activated.T, upstream_low, preferred_element_type=jnp.float32)
    grad_down_bias = column_sums(upstream_low)
    grad_activated = jnp.dot(upstream_low, down_back.T, preferred_element_type=jnp.float32)
    slope = 0.5 * error_part + preacts * jnp.exp(-0.5 * preacts * preacts) * INV_ROOT_TAU
    grad_preacts = (grad_activated * slope).astype(jnp.bfloat16)
    grad_up_weight = jnp.dot(normed_two.T, grad_preacts, preferred_element_type=jnp.float32)
    grad_up_bias = column_sums(grad_preacts)
    grad_normed_two = jnp.dot(grad_preacts, up_back.T, preferred_element_type=jnp.float32)
    grad_mlp_gain = jnp.sum(grad_normed_two * scaled_two, axis=0)
    grad_mlp_shift = jnp.sum(grad_normed_two, axis=0)
    grad_middle = upstream + norm_back(grad_normed_two, gain_two_back, scaled_two, inverse_two)
    grad_branch = grad_middle.astype(jnp.bfloat16)
    grad_out_weight = jnp.dot(context_low.T, grad_branch, preferred_element_type=jnp.float32)
    grad_out_bias = column_sums(grad_branch)
    grad_context = jnp.dot(grad_branch, out_back.T, preferred_element_type=jnp.float32).astype(
        jnp.bfloat16
    )
    grad_projected = lax.cond(
        is_global,
        lambda parts: attend_crops_back(parts[0], parts[1], parts[2], parts[3], parts[4], GLEN),
        lambda parts: attend_crops_back(parts[0], parts[1], parts[2], parts[3], parts[4], LLEN),
        (queries, key_rows, value_rows, logsum, grad_context),
    )
    grad_qkv_weight = jnp.dot(normed_one.T, grad_projected, preferred_element_type=jnp.float32)
    grad_query_bias = column_sums(grad_projected[:, :D])
    grad_value_bias = column_sums(grad_projected[:, 2 * D :])
    grad_normed_one = jnp.dot(grad_projected, qkv_back.T, preferred_element_type=jnp.float32)
    grad_attn_gain = jnp.sum(grad_normed_one * scaled_one, axis=0)
    grad_attn_shift = jnp.sum(grad_normed_one, axis=0)
    grad_tokens = (
        grad_middle + norm_back(grad_normed_one, gain_one_back, scaled_one, inverse_one)
    ).astype(jnp.bfloat16)
    shards = (
        lax.psum_scatter(
            grad_qkv_weight.astype(jnp.bfloat16), "fsdp", scatter_dimension=0, tiled=True
        ).astype(jnp.float32),
        lax.psum_scatter(
            grad_query_bias.astype(jnp.bfloat16), "fsdp", scatter_dimension=0, tiled=True
        ).astype(jnp.float32),
        lax.psum_scatter(
            grad_value_bias.astype(jnp.bfloat16), "fsdp", scatter_dimension=0, tiled=True
        ).astype(jnp.float32),
        lax.psum_scatter(
            grad_out_weight.astype(jnp.bfloat16), "fsdp", scatter_dimension=0, tiled=True
        ).astype(jnp.float32),
        lax.psum_scatter(
            grad_out_bias.astype(jnp.bfloat16), "fsdp", scatter_dimension=0, tiled=True
        ).astype(jnp.float32),
        lax.psum_scatter(
            grad_attn_gain.astype(jnp.bfloat16), "fsdp", scatter_dimension=0, tiled=True
        ).astype(jnp.float32),
        lax.psum_scatter(
            grad_attn_shift.astype(jnp.bfloat16), "fsdp", scatter_dimension=0, tiled=True
        ).astype(jnp.float32),
        lax.psum_scatter(
            grad_mlp_gain.astype(jnp.bfloat16), "fsdp", scatter_dimension=0, tiled=True
        ).astype(jnp.float32),
        lax.psum_scatter(
            grad_mlp_shift.astype(jnp.bfloat16), "fsdp", scatter_dimension=0, tiled=True
        ).astype(jnp.float32),
        lax.psum_scatter(
            grad_up_weight.astype(jnp.bfloat16), "fsdp", scatter_dimension=0, tiled=True
        ).astype(jnp.float32),
        lax.psum_scatter(
            grad_up_bias.astype(jnp.bfloat16), "fsdp", scatter_dimension=0, tiled=True
        ).astype(jnp.float32),
        lax.psum_scatter(
            grad_down_weight.astype(jnp.bfloat16), "fsdp", scatter_dimension=0, tiled=True
        ).astype(jnp.float32),
        lax.psum_scatter(
            grad_down_bias.astype(jnp.bfloat16), "fsdp", scatter_dimension=0, tiled=True
        ).astype(jnp.float32),
    )
    merged = (
        lax.psum(shards[0].astype(jnp.bfloat16), "dp").astype(jnp.float32),
        lax.psum(shards[1].astype(jnp.bfloat16), "dp").astype(jnp.float32),
        lax.psum(shards[2].astype(jnp.bfloat16), "dp").astype(jnp.float32),
        lax.psum(shards[3].astype(jnp.bfloat16), "dp").astype(jnp.float32),
        lax.psum(shards[4].astype(jnp.bfloat16), "dp").astype(jnp.float32),
        lax.psum(shards[5].astype(jnp.bfloat16), "dp").astype(jnp.float32),
        lax.psum(shards[6].astype(jnp.bfloat16), "dp").astype(jnp.float32),
        lax.psum(shards[7].astype(jnp.bfloat16), "dp").astype(jnp.float32),
        lax.psum(shards[8].astype(jnp.bfloat16), "dp").astype(jnp.float32),
        lax.psum(shards[9].astype(jnp.bfloat16), "dp").astype(jnp.float32),
        lax.psum(shards[10].astype(jnp.bfloat16), "dp").astype(jnp.float32),
        lax.psum(shards[11].astype(jnp.bfloat16), "dp").astype(jnp.float32),
        lax.psum(shards[12].astype(jnp.bfloat16), "dp").astype(jnp.float32),
    )
    return (
        mixed_out,
        grad_tokens,
        merged[0],
        merged[1],
        merged[2],
        merged[3],
        merged[4],
        merged[5],
        merged[6],
        merged[7],
        merged[8],
        merged[9],
        merged[10],
        merged[11],
        merged[12],
    )


def solution(mesh):
    placed = (
        P(("dp", "fsdp"), None),
        P(("dp", "fsdp"), None),
        P("dp"),
        P(),
        P("fsdp", None),
        P("fsdp"),
        P("fsdp"),
        P("fsdp", None),
        P("fsdp"),
        P("fsdp"),
        P("fsdp"),
        P("fsdp"),
        P("fsdp"),
        P("fsdp", None),
        P("fsdp"),
        P("fsdp", None),
        P("fsdp"),
    )
    return jax.shard_map(
        local,
        mesh=mesh,
        in_specs=placed,
        out_specs=(
            P(("dp", "fsdp"), None),
            P(("dp", "fsdp"), None),
            P("fsdp", None),
            P("fsdp"),
            P("fsdp"),
            P("fsdp", None),
            P("fsdp"),
            P("fsdp"),
            P("fsdp"),
            P("fsdp"),
            P("fsdp"),
            P("fsdp", None),
            P("fsdp"),
            P("fsdp", None),
            P("fsdp"),
        ),
        check_vma=False,
    )
```

profile of v0, /device:TPU:0, one launch (start us, length us, event | category | flops | bytes accessed | tf_op | source)
XLA Modules:
  0.0 1136.9 jit_solution(5264988869393744086)
XLA Ops:
  23.5 14.1 %all-gather.4 = bf16[4,1,256]{2,1,0:T(2,128)(2,1)S(1)} all-gather(bf16[1,1,256]{2,1,0:T(2,128)(2,1)S(1)} %reshape.192), channel_id=1, replica_groups=mesh['dp'=8,'fsdp'=4] {'fsdp'}, dimensions={0}, use_global_device_ids=true | all-gather | bytes 2560 | tf_op jit(solution)/shard_map/all_gather | solution.py:132
  45.9 9.7 all-gather.2
  55.7 15.9 %all-gather.1 = bf16[4,1,256]{2,1,0:T(2,128)(2,1)S(1)} all-gather(bf16[1,1,256]{2,1,0:T(2,128)(2,1)S(1)} %reshape.186), channel_id=1, replica_groups=mesh['dp'=8,'fsdp'=4] {'fsdp'}, dimensions={0}, use_global_device_ids=true | all-gather | bytes 2560 | tf_op jit(solution)/shard_map/all_gather | solution.py:134
  71.6 8.5 all-gather
  80.1 17.2 %all_gather.55 = bf16[4096]{0:T(1024)(128)(2,1)S(1)} all-gather(bf16[1024]{0:T(1024)(128)(2,1)S(1)} %convert_element_type.280), channel_id=1, replica_groups=mesh['dp'=8,'fsdp'=4] {'fsdp'}, dimensions={0}, use_global_device_ids=true | all-gather | bytes 10240 | tf_op jit(solution)/shard_map/all_gather | solution.py:138
  105.8 17.0 %all-gather.5 = bf16[4,1,256]{2,1,0:T(2,128)(2,1)S(1)} all-gather(bf16[1,1,256]{2,1,0:T(2,128)(2,1)S(1)} %reshape.194), channel_id=1, replica_groups=mesh['dp'=8,'fsdp'=4] {'fsdp'}, dimensions={0}, use_global_device_ids=true | all-gather | bytes 2560 | tf_op jit(solution)/shard_map/all_gather | solution.py:135
  138.1 36.5 %conditional.5 = (f32[600,16]{0,1:T(8,128)S(1)}, bf16[600,1024]{1,0:T(8,128)(2,1)}) conditional(s32[]{:T(128)} %bitcast.12, (bf16[600,1024]{1,0:T(8,128)(2,1)}, bf16[600,1024]{1,0:T(8,128)(2,1)S(1)}, bf16[600,1024]{1,0:T(8,128)(2,1)S(1)}) %tuple.35, (bf16[600,1024]{1,0:T(8,128)(2,1)}, bf16[600,1024]{1,0:T(8,128)(2,1)S(1)}, ...), branch_computations={%region_2.5_spmd, %region_5.8_spmd} | conditional | flops 127804800 | bytes 31104044
  181.0 144.4 %all-gather.17.cloned.1.call-done = bf16[1024,4096]{1,0:T(8,128)(2,1)} async-done(((bf16[256,4096]{1,0:T(8,128)(2,1)}), bf16[1024,4096]{1,0:T(8,128)(2,1)}) %all-gather.17.cloned.1.call-update) | async-done | bytes 8388624 | tf_op jit(solution)/shard_map/all_gather | solution.py:137
  325.3 13.0 %multiply_convert_fusion.2 = (bf16[600,4096]{1,0:T(8,128)(2,1)}, f32[600,4096]{1,0:T(8,128)}) fusion(f32[4096]{0:T(1024)S(1)} %convert_element_type.281, bf16[1024,4096]{1,0:T(8,128)(2,1)} %all-gather.17.cloned.1.call-done, f32[600,1024]{1,0:T(8,128)} %copy-done.16, f32[1024]{0:T(1024)S(1)} %bitcast.93, f32[1024]{0:T(1024)S(1)} %bitcast.81, ...), kind=kOutput, calls=%fused_computation.81 | convolution fusion | flops 5050982400 | bytes 25621184 | tf_op jit(solution)/shard_map/dot_general | solution.py:188
  338.3 136.3 %all-gather.19.cloned.1.call-done = bf16[4096,1024]{1,0:T(8,128)(2,1)} async-done(((bf16[1024,1024]{1,0:T(8,128)(2,1)}), bf16[4096,1024]{1,0:T(8,128)(2,1)}) %all-gather.19.cloned.1.call-update) | async-done | bytes 8388624 | tf_op jit(solution)/shard_map/all_gather | solution.py:139
  474.6 14.1 %fusion.107 = (bf16[4096]{0:T(1024)(128)(2,1)S(1)}, bf16[600,4096]{1,0:T(8,128)(2,1)}) fusion(f32[600,4096]{1,0:T(8,128)} %get-tuple-element.142, f32[4096]{0:T(1024)S(1)} %convert_element_type.281, bf16[4096,1024]{1,0:T(8,128)(2,1)} %all-gather.19.cloned.1.call-done, bf16[600,1024]{1,0:T(8,128)(2,1)} %param.22, f32[]{:T(128)} %bitcast.21), kind=kOutput, calls=%fused_computation.137 | convolution fusion | flops 5064495104 | bytes 24387588 | tf_op jit(solution)/shard_map/dot_general | solution.py:208
  488.7 9.1 multiply_reduce_fusion.4
  509.0 64.7 %conditional.6 = (bf16[600,3072]{1,0:T(8,128)(2,1)}) conditional(s32[]{:T(128)} %bitcast.12, (bf16[600,1024]{1,0:T(8,128)(2,1)}, bf16[600,1024]{1,0:T(8,128)(2,1)S(1)}, f32[600,16]{0,1:T(8,128)S(1)}, bf16[600,1024]{1,0:T(8,128)(2,1)}, bf16[600,1024]{1,0:T(8,128)(2,1)S(1)}) %tuple.36, (bf16[600,1024]{1,0:T(8,128)(2,1)}, ...), branch_computations={%region_12.0_spmd, %region_14.0_spmd} | conditional | flops 326467200 | bytes 103913696
  573.8 9.7 convolution_convert_fusion.2
  585.2 11.6 %convolution_convert_fusion = bf16[1024,4096]{1,0:T(8,128)(2,1)} fusion(bf16[600,4096]{1,0:T(8,128)(2,1)} %get-tuple-element.146, f32[600,1024]{1,0:T(8,128)S(1)} %copy-done.18, f32[1024]{0:T(1024)S(1)} %bitcast.94, f32[1024]{0:T(1024)S(1)} %bitcast.84, f32[600]{0:T(1024)S(1)} %add_rsqrt_fusion, f32[600]{0:T(1024)S(1)} %broadcast_multiply_fusion.4), kind=kOutput, calls=%fused_computation.83 | convolution fusion | flops 5040431104 | bytes 15774400 | tf_op jit(solution)/shard_map/dot_general | solution.py:211
  598.1 11.5 %convolution_convert_fusion.1 = bf16[4096,1024]{1,0:T(8,128)(2,1)} fusion(bf16[600,4096]{1,0:T(8,128)(2,1)} %get-tuple-element.141, bf16[600,1024]{1,0:T(8,128)(2,1)S(1)} %copy-done.26, f32[]{:T(128)} %bitcast.21), kind=kOutput, calls=%fused_computation.84 | convolution fusion | flops 5039202304 | bytes 14532612 | tf_op jit(solution)/shard_map/dot_general | solution.py:206
  620.6 95.7 %reduce-scatter.5.cloned.1.call-done = bf16[256,3072]{1,0:T(8,128)(2,1)} async-done(((bf16[1024,3072]{1,0:T(8,128)(2,1)}), bf16[256,3072]{1,0:T(8,128)(2,1)}) %reduce-scatter.5.cloned.1.call-update) | async-done | bytes 1572880 | tf_op jit(solution)/shard_map/reduce_scatter | solution.py:239
  716.3 147.5 %reduce-scatter.9.cloned.1.call-done = bf16[256,4096]{1,0:T(8,128)(2,1)} async-done(((bf16[1024,4096]{1,0:T(8,128)(2,1)}), bf16[256,4096]{1,0:T(8,128)(2,1)}) %reduce-scatter.9.cloned.1.call-update) | async-done | bytes 2097168 | tf_op jit(solution)/shard_map/reduce_scatter | solution.py:266
  863.9 147.6 %reduce-scatter.11.cloned.1.call-done = bf16[1024,1024]{1,0:T(8,128)(2,1)} async-done(((bf16[4096,1024]{1,0:T(8,128)(2,1)}), bf16[1024,1024]{1,0:T(8,128)(2,1)}) %reduce-scatter.11.cloned.1.call-update) | async-done | bytes 2097168 | tf_op jit(solution)/shard_map/reduce_scatter | solution.py:272
  1012.8 9.8 fusion.93
  1023.0 18.5 %all-reduce.11 = (bf16[1024]{0:T(1024)(128)(2,1)S(1)}, bf16[1024]{0:T(1024)(128)(2,1)S(1)}, bf16[1024]{0:T(1024)(128)(2,1)S(1)}, bf16[1024]{0:T(1024)(128)(2,1)S...) all-reduce(bf16[1024]{0:T(1024)(128)(2,1)S(1)} %get-tuple-element.9, ...), channel_id=3, replica_groups=mesh['dp'=8,'fsdp'=4] {'fsdp'}, use_global_device_ids=true, to_apply=%region_21.22.clone | all-reduce | flops 12288 | bytes 49152
  1042.1 12.7 %all-reduce.9 = (bf16[256]{0:T(256)(128)(2,1)S(1)}, bf16[256]{0:T(256)(128)(2,1)S(1)}, bf16[256]{0:T(256)(128)(2,1)S(1)}, bf16[256]{0:T(256)(128)(2,1)S(1)}, bf1...) all-reduce(bf16[256]{0:T(256)(128)(2,1)S(1)} %dynamic-slice.1, ...), channel_id=1, replica_groups=mesh['dp'=8,'fsdp'=4] {'dp'}, use_global_device_ids=true, to_apply=%region_22.23 | all-reduce | flops 3072 | bytes 12288 | tf_op jit(solution)/shard_map/psum | solution.py:281
  1064.4 10.0 add_convert_fusion.1
  1074.4 45.7 %all-reduce.14.cloned.1.call-done = (bf16[256,3072]{1,0:T(8,128)(2,1)}, bf16[256,1024]{1,0:T(8,128)(2,1)}, bf16[256,4096]{1,0:T(8,128)(2,1)}, bf16[1024,1024]{1,0:T(8,128)(2,1)}) async-done(((bf16[256,3072]{1,0:T(8,128)(2,1)}, bf16[256,1024]{1,0:T(8,128)(2,1)}, bf16[256,4096]{1,0:T(8,128)(2,1)}, bf16[1024,1024]{1,0:T(8,128)(2,1)}), (bf16[256,3072]{1,0:T(8,128)(2,1)}, bf16[256,1024]{1,0:T(8,128)(2,1)}, ...) | async-done | bytes 6291472 | tf_op jit(solution)/shard_map/psum | solution.py:280
  (223 shorter events, 183.6 us)
Async XLA Ops:
  7.2 122.1 %all-gather.13.cloned.1.call-start = ((), (), s32[]{:S(2)}) async-start(), calls=%async_computation.4 | async-start | bytes 7864320 | tf_op jit(solution)/shard_map/all_gather | solution.py:128
  10.6 164.7 %all-gather.15.cloned.1.call-start = ((), (), s32[]{:S(2)}) async-start(), calls=%async_computation.5 | async-start | bytes 2621440 | tf_op jit(solution)/shard_map/all_gather | solution.py:131
  11.5 313.8 %all-gather.17.cloned.1.call-start = ((), (), s32[]{:S(2)}) async-start(), calls=%async_computation.6 | async-start | bytes 10485760 | tf_op jit(solution)/shard_map/all_gather | solution.py:137
  15.4 22.2 %copy-start.44 = (f32[256]{0:T(256)S(1)}, f32[256]{0:T(256)}, u32[]{:S(2)}) copy-start(f32[256]{0:T(256)} %param.27) | copy-start | bytes 3076
  15.4 30.4 %copy-start.45 = (f32[256]{0:T(256)S(1)}, f32[256]{0:T(256)}, u32[]{:S(2)}) copy-start(f32[256]{0:T(256)} %param.26) | copy-start | bytes 3076
  15.4 40.2 %copy-start.46 = (f32[256]{0:T(256)S(1)}, f32[256]{0:T(256)}, u32[]{:S(2)}) copy-start(f32[256]{0:T(256)} %param.31) | copy-start | bytes 3076
  15.5 56.1 %copy-start.47 = (f32[256]{0:T(256)S(1)}, f32[256]{0:T(256)}, u32[]{:S(2)}) copy-start(f32[256]{0:T(256)} %param.30) | copy-start | bytes 3076
  15.5 64.7 %copy-start.35 = (f32[1024]{0:T(1024)S(1)}, f32[1024]{0:T(1024)}, u32[]{:S(2)}) copy-start(f32[1024]{0:T(1024)} %param.35) | copy-start | bytes 12292
  15.5 81.9 %copy-start.48 = (f32[256]{0:T(256)S(1)}, f32[256]{0:T(256)}, u32[]{:S(2)}) copy-start(f32[256]{0:T(256)} %param.33) | copy-start | bytes 3076
  15.5 90.3 %copy-start.49 = (f32[256]{0:T(256)S(1)}, f32[256]{0:T(256)}, u32[]{:S(2)}) copy-start(f32[256]{0:T(256)} %param.32) | copy-start | bytes 3076
  15.5 107.4 %copy-start.12 = (bf16[600,1024]{1,0:T(8,128)(2,1)S(1)}, bf16[600,1024]{1,0:T(8,128)(2,1)}, u32[]{:S(2)}) copy-start(bf16[600,1024]{1,0:T(8,128)(2,1)} %param.21) | copy-start | bytes 3686404
  15.5 459.1 %all-gather.19.cloned.1.call-start = ((), (), s32[]{:S(2)}) async-start(), calls=%async_computation.7 | async-start | bytes 10485760 | tf_op jit(solution)/shard_map/all_gather | solution.py:139
  19.6 601.0 %reduce-scatter.7.cloned.1.call-start = ((), (), s32[]{:S(2)}) async-start(), calls=%async_computation.9 | async-start | bytes 2621440 | tf_op jit(solution)/shard_map/reduce_scatter | solution.py:248
  71.6 57.7 %copy-start.36 = (f32[4,1,256]{2,1,0:T(1,128)}, f32[4,1,256]{2,1,0:T(1,128)S(1)}, u32[]{:S(2)}) copy-start(f32[4,1,256]{2,1,0:T(1,128)S(1)} %convert_element_type.325) | copy-start | bytes 12292
  80.1 49.2 %copy-start.31 = (f32[4,1,256]{2,1,0:T(1,128)}, f32[4,1,256]{2,1,0:T(1,128)S(1)}, u32[]{:S(2)}) copy-start(f32[4,1,256]{2,1,0:T(1,128)S(1)} %convert_element_type.324) | copy-start | bytes 12292
  105.8 219.5 %copy-start.37 = (f32[4,1,256]{2,1,0:T(1,128)}, f32[4,1,256]{2,1,0:T(1,128)S(1)}, u32[]{:S(2)}) copy-start(f32[4,1,256]{2,1,0:T(1,128)S(1)} %convert_element_type.330) | copy-start | bytes 12292
  474.6 14.1 %copy-start.42 = (bf16[1024,4096]{1,0:T(8,128)(2,1)S(1)}, bf16[1024,4096]{1,0:T(8,128)(2,1)}, u32[]{:S(2)}) copy-start(bf16[1024,4096]{1,0:T(8,128)(2,1)} %all-gather.17.cloned.1.call-done) | copy-start | bytes 25165828
  504.1 212.3 %reduce-scatter.5.cloned.1.call-start = ((), (), s32[]{:S(2)}) async-start(), calls=%async_computation.8 | async-start | bytes 7864320 | tf_op jit(solution)/shard_map/reduce_scatter | solution.py:239
  509.0 64.8 %copy-start.30 = (f32[600]{0:T(1024)S(1)}, f32[600]{0:T(1024)}, u32[]{:S(2)}) copy-start(f32[600]{0:T(1024)} %copy-done.29) | copy-start | bytes 7204
  509.0 64.8 %copy-start.32 = (f32[4,1,256]{2,1,0:T(1,128)S(1)}, f32[4,1,256]{2,1,0:T(1,128)}, u32[]{:S(2)}) copy-start(f32[4,1,256]{2,1,0:T(1,128)} %copy-done.31) | copy-start | bytes 12292
  509.0 64.8 %copy-start.34 = (f32[600]{0:T(1024)S(1)}, f32[600]{0:T(1024)}, u32[]{:S(2)}) copy-start(f32[600]{0:T(1024)} %copy-done.33) | copy-start | bytes 7204
  583.5 280.3 %reduce-scatter.9.cloned.1.call-start = ((), (), s32[]{:S(2)}) async-start(), calls=%async_computation.10 | async-start | bytes 10485760 | tf_op jit(solution)/shard_map/reduce_scatter | solution.py:266
  596.8 414.6 %reduce-scatter.11.cloned.1.call-start = ((), (), s32[]{:S(2)}) async-start(), calls=%async_computation.11 | async-start | bytes 10485760 | tf_op jit(solution)/shard_map/reduce_scatter | solution.py:272
  609.6 510.6 %all-reduce.14.cloned.1.call-start = ((), (), s32[]{:S(2)}) async-start(), calls=%async_computation.12 | async-start | bytes 12582912 | tf_op jit(solution)/shard_map/psum | solution.py:280
  (32 other events, 162.4 us)
Sparse Core Ops, SparseCore 0:
  10.7 118.5 all-gather.12
  131.4 43.8 all-gather.14
  176.9 148.4 all-gather.16
  326.7 147.7 all-gather.18
  504.2 41.7 reduce-scatter.6
  583.6 132.6 reduce-scatter.4
  718.7 145.1 reduce-scatter.8
  866.2 145.2 reduce-scatter.10
  1015.1 105.0 all-reduce.13
where the time goes:
time: 1140 us
  waiting for transfers between devices  724 us (64%)
  matrix products  141 us (12%)
  blocking collectives  139 us (12%)
  local copies, waits for them, and re-layouts  58.2 us (5%)
  other arithmetic  41.2 us (4%)
  between operations  19.5 us (2%)
  loops' own time  14.1 us (1%)
    reduce_scatter x1, waiting for transfers between devices, local(): lax.psum_scatter(grad_down_weight.astype(jnp.bfloat16), 'fsdp', scatter_d...  148 us
    reduce_scatter x1, waiting for transfers between devices, local(): lax.psum_scatter(grad_up_weight.astype(jnp.bfloat16), 'fsdp', scatter_dim...  148 us
    all_gather x1, waiting for transfers between devices, local(): lax.all_gather(up_weight.astype(jnp.bfloat16), 'fsdp', axis=0, tiled=True)  144 us
    all_gather x1, waiting for transfers between devices, local(): lax.all_gather(down_weight.astype(jnp.bfloat16), 'fsdp', axis=0, tiled=True)  136 us
    reduce_scatter x1, waiting for transfers between devices, local(): lax.psum_scatter(grad_qkv_weight.astype(jnp.bfloat16), 'fsdp', scatter_di...  95.7 us
    psum x1, waiting for transfers between devices, local(): lax.psum(shards[0].astype(jnp.bfloat16), 'dp').astype(jnp.float32)  45.7 us
    reshape x7, local copies, waits for them, and re-layouts, by_crops(): return values.reshape(values.shape[0] // crop, crop, HEADS, HEAD_DIM)  24.5 us
  transfers between devices with their start and end apart: 9, of which 8 were waited for; matrix products, arithmetic and copies ran while one was open for 17% of the time, Pallas kernels for 0%

commit v1 on v0

v1 whole, which is shorter than its diff:
```python
import functools

import jax
import jax.numpy as jnp
from jax import lax
from jax.sharding import PartitionSpec as P

D = 1024
HEADS = 16
HEAD_DIM = 64
GLEN = 50
LLEN = 10


EPSILON = 1e-06
ROOT_HALF = 0.7071067811865476
INV_ROOT_TAU = 0.3989422804014327


def normalize(values):
    middle = jnp.mean(values, axis=-1, keepdims=True)
    centered = values - middle
    inverse = lax.rsqrt(jnp.mean(centered * centered, axis=-1, keepdims=True) + EPSILON)
    return (centered * inverse, inverse)


def norm_back(grad_out, gain, scaled, inverse):
    grad_scaled = grad_out * gain
    return inverse * (
        grad_scaled
        - jnp.mean(grad_scaled, axis=-1, keepdims=True)
        - scaled * jnp.mean(grad_scaled * scaled, axis=-1, keepdims=True)
    )


def by_crops(values, crop):
    return values.reshape(values.shape[0] // crop, crop, HEADS, HEAD_DIM)


def crop_scores(queries, key_rows):
    factor = HEAD_DIM ** (-0.5)
    return (
        jnp.einsum("cqhd,ckhd->chqk", queries, key_rows, preferred_element_type=jnp.float32)
        * factor
    )


def attend_crops(queries, key_rows, value_rows, crop):
    length = queries.shape[0]
    crop_q, crop_k, crop_v = (
        by_crops(queries, crop),
        by_crops(key_rows, crop),
        by_crops(value_rows, crop),
    )
    scores = crop_scores(crop_q, crop_k)
    highest = jnp.max(scores, axis=-1, keepdims=True)
    exponent = jnp.exp(scores - highest)
    summed = jnp.sum(exponent, axis=-1, keepdims=True)
    attention = (exponent / summed).astype(jnp.bfloat16)
    context = jnp.einsum("chqk,ckhd->cqhd", attention, crop_v, preferred_element_type=jnp.float32)
    logsum = (highest + jnp.log(summed))[..., 0]
    return (
        context.reshape(length, HEADS * HEAD_DIM),
        jnp.transpose(logsum, (0, 2, 1)).reshape(length, HEADS),
    )


def attend_crops_back(queries, key_rows, value_rows, logsum, grad_context, crop):
    length = queries.shape[0]
    factor = HEAD_DIM ** (-0.5)
    crop_q, crop_k, crop_v = (
        by_crops(queries, crop),
        by_crops(key_rows, crop),
        by_crops(value_rows, crop),
    )
    crop_g = by_crops(grad_context, crop)
    crop_l = jnp.transpose(logsum.reshape(length // crop, crop, HEADS), (0, 2, 1))
    scores = crop_scores(crop_q, crop_k)
    probs = jnp.exp(scores - crop_l[..., None])
    probs_low = probs.astype(jnp.bfloat16)
    grad_values = jnp.einsum(
        "chqk,cqhd->ckhd", probs_low, crop_g, preferred_element_type=jnp.float32
    )
    grad_probs = jnp.einsum("cqhd,ckhd->chqk", crop_g, crop_v, preferred_element_type=jnp.float32)
    delta = jnp.sum(probs * grad_probs, axis=-1, keepdims=True)
    grad_scores = (probs * (grad_probs - delta)).astype(jnp.bfloat16)
    grad_queries = (
        jnp.einsum("chqk,ckhd->cqhd", grad_scores, crop_k, preferred_element_type=jnp.float32)
        * factor
    )
    grad_keys = (
        jnp.einsum("chqk,cqhd->ckhd", grad_scores, crop_q, preferred_element_type=jnp.float32)
        * factor
    )
    width = HEADS * HEAD_DIM
    return jnp.concatenate(
        [
            grad_queries.reshape(length, width),
            grad_keys.reshape(length, width),
            grad_values.reshape(length, width),
        ],
        axis=1,
    ).astype(jnp.bfloat16)


VECTOR_ORDER = (1, 2, 4, 5, 6, 7, 8, 10, 12)


def xor_pairs(n, mask):
    return [(i, i ^ mask) for i in range(n)]


def ring_pairs(n):
    return [(i, (i + 1) % n) for i in range(n)]


def chip_masks(n_dp):
    masks = []
    mask = 2
    while mask < n_dp:
        masks.append(mask)
        mask *= 2
    return masks


def spread_in_plane(items, n_dp, order):
    held = list(items)
    batches = [list(items)]
    for mask in order:
        got = lax.ppermute([it[2] for it in held], "dp", xor_pairs(n_dp, mask))
        new = [(it[0] ^ mask, it[1], piece) for it, piece in zip(held, got)]
        held = held + new
        batches.append(new)
    partner = []
    for batch in batches:
        got = lax.ppermute([it[2] for it in batch], "dp", xor_pairs(n_dp, 1))
        partner += [(it[0] ^ 1, it[1], piece) for it, piece in zip(batch, got)]
    return held + partner


def gather_weights(shards, n_dp, n_fsdp):
    d = lax.axis_index("dp")
    f = lax.axis_index("fsdp")
    rows = [s.shape[0] // (2 * n_dp) for s in shards]
    full = [
        lax.dynamic_update_slice(
            jnp.zeros((n_fsdp, n_dp, 2, r, s.shape[1]), s.dtype),
            s.reshape(1, n_dp, 2, r, s.shape[1]),
            (f, 0, 0, 0, 0),
        )
        for s, r in zip(shards, rows)
    ]
    own = [
        [lax.dynamic_slice_in_dim(s, (2 * d + h) * r, r, 0) for s, r in zip(shards, rows)]
        for h in range(2)
    ]
    z_items = ([], [])
    buf = own
    for step in range(1, n_fsdp):
        buf = lax.ppermute(buf, "fsdp", ring_pairs(n_fsdp))
        source = (f - step) % n_fsdp
        for h in range(2):
            z_items[h].append((0, source, buf[h]))
    masks = chip_masks(n_dp)
    for h in range(2):
        order = masks if h == 0 else masks[::-1]
        for x, source, pieces in spread_in_plane(z_items[h], n_dp, order):
            full = [
                lax.dynamic_update_slice(w, p[None, None, None], (source, d ^ x, h, 0, 0))
                for w, p in zip(full, pieces)
            ]
    return [w.reshape(-1, w.shape[-1]) for w in full]


def reduce_weights(grads, n_dp, n_fsdp):
    d = lax.axis_index("dp")
    f = lax.axis_index("fsdp")
    bits = n_dp.bit_length() - 1
    rows = [g.shape[0] // (n_fsdp * 2 * n_dp) for g in grads]
    masks = chip_masks(n_dp)
    finals = []
    for h in range(2):
        acc = [
            g.reshape((n_fsdp,) + (2,) * bits + (2, r, g.shape[1]))[(slice(None),) * (bits + 1) + (h,)]
            for g, r in zip(grads, rows)
        ]
        live = list(range(bits - 1, -1, -1))
        seq = [1] + (masks[::-1] if h == 0 else masks)
        for mask in seq:
            bit = mask.bit_length() - 1
            axis = 1 + live.index(bit)
            mine = (d >> bit) & 1
            send = [lax.dynamic_index_in_dim(a, 1 - mine, axis, keepdims=False) for a in acc]
            keep = [lax.dynamic_index_in_dim(a, mine, axis, keepdims=False) for a in acc]
            got = lax.ppermute([s.astype(jnp.bfloat16) for s in send], "dp", xor_pairs(n_dp, mask))
            acc = [k.astype(jnp.float32) + g.astype(jnp.float32) for k, g in zip(keep, got)]
            live.remove(bit)
        if n_fsdp == 1:
            finals.append([a[0].astype(jnp.bfloat16) for a in acc])
            continue
        send = [lax.dynamic_index_in_dim(a, (f - 1) % n_fsdp, 0, keepdims=False).astype(jnp.bfloat16) for a in acc]
        for step in range(1, n_fsdp):
            got = lax.ppermute(send, "fsdp", ring_pairs(n_fsdp))
            chunk = (f - 1 - step) % n_fsdp
            send = [
                (g.astype(jnp.float32) + lax.dynamic_index_in_dim(a, chunk, 0, keepdims=False)).astype(jnp.bfloat16)
                for g, a in zip(got, acc)
            ]
        finals.append(send)
    outs = [jnp.zeros((n_dp, 2, r, g.shape[1]), jnp.bfloat16) for g, r in zip(grads, rows)]
    for h in range(2):
        order = masks if h == 0 else masks[::-1]
        for x, _, pieces in spread_in_plane([(0, None, finals[h])], n_dp, order):
            outs = [lax.dynamic_update_slice(o, p[None, None], (d ^ x, h, 0, 0)) for o, p in zip(outs, pieces)]
    return [o.reshape(-1, o.shape[-1]).astype(jnp.float32) for o in outs]


def gather_weights_native(shards, n_dp, n_fsdp):
    return [lax.all_gather(s, "fsdp", axis=0, tiled=True) for s in shards]


def reduce_weights_native(grads, n_dp, n_fsdp):
    return [
        lax.psum(lax.psum_scatter(g, "fsdp", scatter_dimension=0, tiled=True), "dp").astype(jnp.float32)
        for g in grads
    ]


def pack_vectors(vectors, n_dp, n_fsdp):
    rows = jnp.concatenate([v.reshape(n_fsdp, -1) for v in vectors], axis=1)
    return rows.reshape(n_fsdp * 2 * n_dp, -1)


def unpack_vectors(packed, sizes, n_fsdp):
    rows = packed.reshape(n_fsdp, -1)
    out = []
    offset = 0
    for size in sizes:
        width = size // n_fsdp
        out.append(rows[:, offset : offset + width].reshape(size))
        offset += width
    return out


def column_sums(values):
    return jnp.sum(values.astype(jnp.float32), axis=0)

def local(
    tokens,
    cotangent,
    crop_group,
    group_tokens,
    qkv_weight,
    query_bias,
    value_bias,
    out_weight,
    out_bias,
    attn_gain,
    attn_shift,
    mlp_gain,
    mlp_shift,
    up_weight,
    up_bias,
    down_weight,
    down_bias,
    n_dp,
    n_fsdp,
):
    small = n_dp * n_fsdp <= 64
    gather = gather_weights if small else gather_weights_native
    reduce = reduce_weights if small else reduce_weights_native
    vectors = (query_bias, value_bias, out_bias, attn_gain, attn_shift, mlp_gain, mlp_shift, up_bias, down_bias)
    sizes = [v.shape[0] * n_fsdp for v in vectors]
    vec_shard = jnp.concatenate([v.astype(jnp.bfloat16) for v in vectors]).reshape(2 * n_dp, -1)
    qkv_low, vec_full = gather([qkv_weight.astype(jnp.bfloat16), vec_shard], n_dp, n_fsdp)
    (out_low,) = gather([out_weight.astype(jnp.bfloat16)], n_dp, n_fsdp)
    (up_low,) = gather([up_weight.astype(jnp.bfloat16)], n_dp, n_fsdp)
    (down_low,) = gather([down_weight.astype(jnp.bfloat16)], n_dp, n_fsdp)
    (
        query_add,
        value_add,
        out_add,
        gain_one,
        shift_one,
        gain_two,
        shift_two,
        up_add,
        down_add,
    ) = [v.astype(jnp.float32) for v in unpack_vectors(vec_full, sizes, n_fsdp)]
    is_global = crop_group[0] == 1
    totals = (group_tokens[0] + group_tokens[1]).astype(jnp.float32)
    loss_share = jnp.where(is_global, group_tokens[1], group_tokens[0]).astype(jnp.float32) / totals
    inputs = tokens.astype(jnp.float32)
    scaled_one, inverse_one = normalize(inputs)
    normed_one = (scaled_one * gain_one + shift_one).astype(jnp.bfloat16)
    projected = jnp.dot(normed_one, qkv_low, preferred_element_type=jnp.float32)
    projected = projected + jnp.concatenate([query_add, jnp.zeros_like(query_add), value_add])
    projected_low = projected.astype(jnp.bfloat16)
    queries = projected_low[:, :D]
    key_rows = projected_low[:, D : 2 * D]
    value_rows = projected_low[:, 2 * D :]
    context, logsum = lax.cond(
        is_global,
        lambda parts: attend_crops(parts[0], parts[1], parts[2], GLEN),
        lambda parts: attend_crops(parts[0], parts[1], parts[2], LLEN),
        (queries, key_rows, value_rows),
    )
    context_low = context.astype(jnp.bfloat16)
    middle = inputs + (jnp.dot(context_low, out_low, preferred_element_type=jnp.float32) + out_add)
    scaled_two, inverse_two = normalize(middle)
    normed_two = (scaled_two * gain_two + shift_two).astype(jnp.bfloat16)
    preacts = jnp.dot(normed_two, up_low, preferred_element_type=jnp.float32) + up_add
    error_part = 1.0 + jax.scipy.special.erf(preacts * ROOT_HALF)
    activated = (0.5 * preacts * error_part).astype(jnp.bfloat16)
    mixed_out = (
        middle + (jnp.dot(activated, down_low, preferred_element_type=jnp.float32) + down_add)
    ).astype(jnp.bfloat16)
    upstream = cotangent.astype(jnp.float32) * loss_share
    upstream_low = upstream.astype(jnp.bfloat16)
    grad_down_weight = jnp.dot(activated.T, upstream_low, preferred_element_type=jnp.float32)
    grad_down_bias = column_sums(upstream_low)
    grad_activated = jnp.dot(upstream_low, down_low.T, preferred_element_type=jnp.float32)
    slope = 0.5 * error_part + preacts * jnp.exp(-0.5 * preacts * preacts) * INV_ROOT_TAU
    grad_preacts = (grad_activated * slope).astype(jnp.bfloat16)
    grad_up_weight = jnp.dot(normed_two.T, grad_preacts, preferred_element_type=jnp.float32)
    grad_up_bias = column_sums(grad_preacts)
    grad_normed_two = jnp.dot(grad_preacts, up_low.T, preferred_element_type=jnp.float32)
    grad_mlp_gain = jnp.sum(grad_normed_two * scaled_two, axis=0)
    grad_mlp_shift = jnp.sum(grad_normed_two, axis=0)
    grad_middle = upstream + norm_back(grad_normed_two, gain_two, scaled_two, inverse_two)
    grad_branch = grad_middle.astype(jnp.bfloat16)
    grad_out_weight = jnp.dot(context_low.T, grad_branch, preferred_element_type=jnp.float32)
    grad_out_bias = column_sums(grad_branch)
    grad_context = jnp.dot(grad_branch, out_low.T, preferred_element_type=jnp.float32).astype(
        jnp.bfloat16
    )
    grad_projected = lax.cond(
        is_global,
        lambda parts: attend_crops_back(parts[0], parts[1], parts[2], parts[3], parts[4], GLEN),
        lambda parts: attend_crops_back(parts[0], parts[1], parts[2], parts[3], parts[4], LLEN),
        (queries, key_rows, value_rows, logsum, grad_context),
    )
    grad_qkv_weight = jnp.dot(normed_one.T, grad_projected, preferred_element_type=jnp.float32)
    grad_query_bias = column_sums(grad_projected[:, :D])
    grad_value_bias = column_sums(grad_projected[:, 2 * D :])
    grad_normed_one = jnp.dot(grad_projected, qkv_low.T, preferred_element_type=jnp.float32)
    grad_attn_gain = jnp.sum(grad_normed_one * scaled_one, axis=0)
    grad_attn_shift = jnp.sum(grad_normed_one, axis=0)
    grad_tokens = (
        grad_middle + norm_back(grad_normed_one, gain_one, scaled_one, inverse_one)
    ).astype(jnp.bfloat16)
    grad_vectors = (
        grad_query_bias,
        grad_value_bias,
        grad_out_bias,
        grad_attn_gain,
        grad_attn_shift,
        grad_mlp_gain,
        grad_mlp_shift,
        grad_up_bias,
        grad_down_bias,
    )
    vec_grads = pack_vectors([g.astype(jnp.bfloat16) for g in grad_vectors], n_dp, n_fsdp)
    (grad_down_shard,) = reduce([grad_down_weight.astype(jnp.bfloat16)], n_dp, n_fsdp)
    (grad_up_shard,) = reduce([grad_up_weight.astype(jnp.bfloat16)], n_dp, n_fsdp)
    (grad_out_shard,) = reduce([grad_out_weight.astype(jnp.bfloat16)], n_dp, n_fsdp)
    grad_qkv_shard, vec_shard_grads = reduce(
        [grad_qkv_weight.astype(jnp.bfloat16), vec_grads], n_dp, n_fsdp
    )
    vec_out = unpack_vectors(vec_shard_grads.reshape(1, -1), [s // n_fsdp for s in sizes], 1)
    return (
        mixed_out,
        grad_tokens,
        grad_qkv_shard,
        vec_out[0],
        vec_out[1],
        grad_out_shard,
        vec_out[2],
        vec_out[3],
        vec_out[4],
        vec_out[5],
        vec_out[6],
        grad_up_shard,
        vec_out[7],
        grad_down_shard,
        vec_out[8],
    )


def solution(mesh):
    placed = (
        P(("dp", "fsdp"), None),
        P(("dp", "fsdp"), None),
        P("dp"),
        P(),
        P("fsdp", None),
        P("fsdp"),
        P("fsdp"),
        P("fsdp", None),
        P("fsdp"),
        P("fsdp"),
        P("fsdp"),
        P("fsdp"),
        P("fsdp"),
        P("fsdp", None),
        P("fsdp"),
        P("fsdp", None),
        P("fsdp"),
    )
    n_dp = mesh.shape["dp"]
    n_fsdp = mesh.shape["fsdp"]
    return jax.shard_map(
        functools.partial(local, n_dp=n_dp, n_fsdp=n_fsdp),
        mesh=mesh,
        in_specs=placed,
        out_specs=(
            P(("dp", "fsdp"), None),
            P(("dp", "fsdp"), None),
            P("fsdp", None),
            P("fsdp"),
            P("fsdp"),
            P("fsdp", None),
            P("fsdp"),
            P("fsdp"),
            P("fsdp"),
            P("fsdp"),
            P("fsdp"),
            P("fsdp", None),
            P("fsdp"),
            P("fsdp", None),
            P("fsdp"),
        ),
        check_vma=False,
    )
```

time: 1140 us -> 1310 us (1.15)
  starting transfers between devices: 0.37 us -> 198 us
  local copies, waits for them, and re-layouts: 58.2 us -> 251 us
  blocking collectives: 139 us -> 0 us
  waiting for transfers between devices: 724 us -> 641 us
    ppermute x0 -> x370, waiting for transfers between devices: none -> 641 us  [the longest x120 271 us: spread_in_plane(): got = lax.ppermute([it[2] for it in held], 'dp', xor_pairs(n_dp, mask))]
    reduce_scatter x4 -> x0, waiting for transfers between devices: 391 us -> none  [the longest x1 148 us: local(): lax.psum_scatter(grad_down_weight.astype(jnp.bfloat16), 'fsdp', scatter_d...]
    all_gather x4 -> x0, waiting for transfers between devices: 287 us -> none  [the longest x1 144 us: local(): lax.all_gather(up_weight.astype(jnp.bfloat16), 'fsdp', axis=0, tiled=True)]
    ppermute x0 -> x370, starting transfers between devices: none -> 198 us  [the longest x120 120 us: spread_in_plane(): got = lax.ppermute([it[2] for it in held], 'dp', xor_pairs(n_dp, mask))]
    dynamic_update_slice x0 -> x315, local copies, waits for them, and re-layouts: none -> 137 us  [the longest x240 134 us: gather_weights(): lax.dynamic_update_slice(w, p[None, None, None], (source, d ^ x, h, 0, 0))]
    all_gather x9 -> x0, blocking collectives: 108 us -> none  [the longest x1 17.2 us: local(): lax.all_gather(up_bias.astype(jnp.bfloat16), 'fsdp', axis=0, tiled=True)]
    psum x1 -> x0, waiting for transfers between devices: 45.7 us -> none  [local(): lax.psum(shards[0].astype(jnp.bfloat16), 'dp').astype(jnp.float32)]
    unnamed x1 -> x0, blocking collectives: 18.5 us -> none
  transfers between devices with their start and end apart: 9 -> 370, of which waited for: 8 -> 257; matrix products, arithmetic and copies ran while one was open for 17% -> 20% of each run, Pallas kernels for 0% -> 0%
where the time goes in v1:
time: 1310 us; the launch traced here: 1300 us
  waiting for transfers between devices  641 us (49%)
  local copies, waits for them, and re-layouts  251 us (19%)
  starting transfers between devices  198 us (15%)
  matrix products  138 us (11%)
  other arithmetic  53.7 us (4%)
  loops' own time  14.1 us (1%)
    ppermute x120, waiting for transfers between devices, spread_in_plane(): got = lax.ppermute([it[2] for it in held], 'dp', xor_pairs(n_dp, mask))  271 us
    dynamic_update_slice x240, local copies, waits for them, and re-layouts, gather_weights(): lax.dynamic_update_slice(w, p[None, None, None], (source, d ^ x, h, 0, 0))  134 us
    ppermute x30, waiting for transfers between devices, reduce_weights(): got = lax.ppermute(send, 'fsdp', ring_pairs(n_fsdp))  127 us
    ppermute x120, starting transfers between devices, spread_in_plane(): got = lax.ppermute([it[2] for it in held], 'dp', xor_pairs(n_dp, mask))  120 us
    ppermute x30, waiting for transfers between devices, reduce_weights(): lax.ppermute([s.astype(jnp.bfloat16) for s in send], 'dp', xor_pairs(n_dp...  100 us
    ppermute x30, waiting for transfers between devices, gather_weights(): buf = lax.ppermute(buf, 'fsdp', ring_pairs(n_fsdp))  80.4 us
    ppermute x160, waiting for transfers between devices, spread_in_plane(): got = lax.ppermute([it[2] for it in batch], 'dp', xor_pairs(n_dp, 1))  62.6 us
    ppermute x160, starting transfers between devices, spread_in_plane(): got = lax.ppermute([it[2] for it in batch], 'dp', xor_pairs(n_dp, 1))  28.5 us
  transfers between devices with their start and end apart: 370, of which 257 were waited for; matrix products, arithmetic and copies ran while one was open for 20% of the time, Pallas kernels for 0%

profile of v1, /device:TPU:0, one launch (start us, length us, event | category | flops | bytes accessed | tf_op | source)
XLA Modules:
  0.0 1302.4 jit_solution(10965014509493725529)
XLA Ops:
  229.3 7.0 collective-permute-done.145
  417.1 10.5 collective-permute-start.169
  470.1 7.3 add_convert_fusion
  478.9 36.9 %conditional.6 = (f32[600,16]{0,1:T(8,128)S(1)}, bf16[600,1024]{1,0:T(8,128)(2,1)}) conditional(s32[]{:T(128)} %bitcast.12, (bf16[600,1024]{1,0:T(8,128)(2,1)}, bf16[600,1024]{1,0:T(8,128)(2,1)S(1)}, bf16[600,1024]{1,0:T(8,128)(2,1)S(1)}) %tuple.48, (bf16[600,1024]{1,0:T(8,128)(2,1)}, bf16[600,1024]{1,0:T(8,128)(2,1)S(1)}, ...), branch_computations={%region_2.5_spmd, %region_5.8_spmd} | conditional | flops 127804800 | bytes 31104044
  628.1 11.9 multiply_convert_fusion.2
  681.9 14.6 %fusion.222 = (bf16[4096]{0:T(1024)(128)(2,1)}, bf16[600,4096]{1,0:T(8,128)(2,1)}) fusion(f32[600,4096]{1,0:T(8,128)} %get-tuple-element.216, f32[4096]{0:T(1024)S(1)} %bitcast.1073, bf16[4096,1024]{1,0:T(8,128)(2,1)} %bitcast.261, bf16[600,1024]{1,0:T(8,128)(2,1)S(1)} %copy-done.50, f32[]{:T(128)} %bitcast.262), kind=kOutput, calls=%fused_computation.667 | convolution fusion | flops 5064495104 | bytes 24387588 | tf_op jit(solution)/shard_map/dot_general | solution.py:322
  696.4 9.1 multiply_reduce_fusion.4
  709.7 91.5 %conditional.8 = (bf16[4,256]{1,0:T(4,128)(2,1)S(1)}, bf16[4,256]{1,0:T(4,128)(2,1)S(1)}, bf16[600,3072]{1,0:T(8,128)(2,1)}) conditional(s32[]{:T(128)} %bitcast.12, (bf16[600,1024]{1,0:T(8,128)(2,1)}, bf16[600,1024]{1,0:T(8,128)(2,1)S(1)}, f32[600,16]{0,1:T(8,128)S(1)}, bf16[600,1024]{1,0:T(8,128)(2,1)}, ...), branch_computations={%region_12.16_spmd, %region_16.20_spmd} | conditional | flops 316634752 | bytes 101468368
  719.6 7.0 fusion.29
  735.9 11.5 multiply_reduce_fusion.2
  747.4 6.9 multiply_convert_fusion
  801.2 10.1 fusion.93
  820.7 9.4 convolution_convert_fusion
  830.1 9.1 convolution_convert_fusion.1
  839.2 8.6 add_convert_fusion.1
  957.0 6.9 collective-permute-done.293
  1067.1 7.7 collective-permute-done.241
  1078.9 50.6 %collective-permute-done.242 = bf16[4,16,3072]{2,1,0:T(8,128)(2,1)S(1)} collective-permute-done((bf16[4,16,3072]{2,1,0:T(8,128)(2,1)S(1)}, bf16[4,16,3072]{2,1,0:T(8,128)(2,1)S(1)}, u32[]{:S(2)}, u32[]{:S(2)}) %collective-permute-start.242) | collective-permute-done | bytes 393248 | tf_op jit(solution)/shard_map/ppermute | solution.py:195
  1131.0 8.4 collective-permute-done.255
  1145.9 6.4 collective-permute-done.256
  1152.3 7.4 collective-permute-done.244
  1159.7 6.6 collective-permute-done.257
  1166.3 6.4 collective-permute-done.245
  1180.6 13.7 %collective-permute-done.248 = bf16[16,3072]{1,0:T(8,128)(2,1)S(1)} collective-permute-done((bf16[16,3072]{1,0:T(8,128)(2,1)S(1)}, bf16[16,3072]{1,0:T(8,128)(2,1)S(1)}, u32[]{:S(2)}, u32[]{:S(2)}) %collective-permute-start.248) | collective-permute-done | bytes 98336 | tf_op jit(solution)/shard_map/ppermute | solution.py:130
  (1506 shorter events, 1044.3 us)
Async XLA Ops:
  16.4 106.9 %collective-permute-start.48 = (bf16[16,3072]{1,0:T(8,128)(2,1)}, bf16[16,3072]{1,0:T(8,128)(2,1)}, u32[]{:S(2)}, u32[]{:S(2)}) collective-permute-start(bf16[16,3072]{1,0:T(8,128)(2,1)} %get-tuple-element.187), channel_id=1, source_target_pairs={{0,1},{1,2},{2,3},{3,0},{4,5},{5,6},{6,7},{7,4},{8,9},{9,10},{10,1... | collective-permute-start | bytes 294920 | tf_op jit(solution)/shard_map/ppermute | solution.py:160
  69.2 221.8 %collective-permute-start.72 = (bf16[16,3072]{1,0:T(8,128)(2,1)}, bf16[16,3072]{1,0:T(8,128)(2,1)S(1)}, u32[]{:S(2)}, u32[]{:S(2)}) collective-permute-start(bf16[16,3072]{1,0:T(8,128)(2,1)} %get-tuple-element.186), channel_id=1, source_target_pairs={{0,1},{1,2},{2,3},{3,0},{4,5},{5,6},{6,7},{7,4},{8,9},{9,10},{10,1... | collective-permute-start | bytes 294920 | tf_op jit(solution)/shard_map/ppermute | solution.py:160
  122.7 291.4 %collective-permute-start.168 = (bf16[16,4096]{1,0:T(8,128)(2,1)S(1)}, bf16[16,4096]{1,0:T(8,128)(2,1)}, u32[]{:S(2)}, u32[]{:S(2)}) collective-permute-start(bf16[16,4096]{1,0:T(8,128)(2,1)S(1)} %get-tuple-element.184), channel_id=1, source_target_pairs={{0,1},{1,2},{2,3},{3,0},{4,5},{5,6},{6,7},{7,4},{8,9},{9,10},{10,1... | collective-permute-start | bytes 393224 | tf_op jit(solution)/shard_map/ppermute | solution.py:160
  124.8 433.6 %collective-permute-start.216 = (bf16[64,1024]{1,0:T(8,128)(2,1)}, bf16[64,1024]{1,0:T(8,128)(2,1)}, u32[]{:S(2)}, u32[]{:S(2)}) collective-permute-start(bf16[64,1024]{1,0:T(8,128)(2,1)} %get-tuple-element.182), channel_id=1, source_target_pairs={{0,1},{1,2},{2,3},{3,0},{4,5},{5,6},{6,7},{7,4},{8,9},{9,10},{10,1... | collective-permute-start | bytes 393224 | tf_op jit(solution)/shard_map/ppermute | solution.py:160
  294.3 103.9 %collective-permute-start.73 = (bf16[16,3072]{1,0:T(8,128)(2,1)S(1)}, bf16[16,3072]{1,0:T(8,128)(2,1)S(1)}, u32[]{:S(2)}, u32[]{:S(2)}) collective-permute-start(bf16[16,3072]{1,0:T(8,128)(2,1)S(1)} %collective-permute-done.72), channel_id=1, source_target_pairs={{0,1},{1,2},{2,3},{3,0},{4,5},{5,6},{6,7},{7,4},{8,9},{9,10},{10,1... | collective-permute-start | bytes 294920 | tf_op jit(solution)/shard_map/ppermute | solution.py:160
  319.5 87.8 %collective-permute-start.75 = (bf16[16,3072]{1,0:T(8,128)(2,1)S(1)}, bf16[16,3072]{1,0:T(8,128)(2,1)S(1)}, u32[]{:S(2)}, u32[]{:S(2)}) collective-permute-start(bf16[16,3072]{1,0:T(8,128)(2,1)S(1)} %collective-permute-done.72), channel_id=1, source_target_pairs={{0,16},{4,20},{8,24},{12,28},{16,0},{20,4},{24,8},{28,12},{1,17},{... | collective-permute-start | bytes 294920 | tf_op jit(solution)/shard_map/ppermute | solution.py:130
  414.1 108.9 %collective-permute-start.156 = (bf16[16,4096]{1,0:T(8,128)(2,1)}, bf16[16,4096]{1,0:T(8,128)(2,1)}, u32[]{:S(2)}, u32[]{:S(2)}) collective-permute-start(bf16[16,4096]{1,0:T(8,128)(2,1)} %collective-permute-done.144), channel_id=1, source_target_pairs={{0,4},{4,0},{8,12},{12,8},{16,20},{20,16},{24,28},{28,24},{1,5},{5... | collective-permute-start | bytes 393224 | tf_op jit(solution)/shard_map/ppermute | solution.py:136
  417.1 141.7 %collective-permute-start.169 = (bf16[16,4096]{1,0:T(8,128)(2,1)}, bf16[16,4096]{1,0:T(8,128)(2,1)}, u32[]{:S(2)}, u32[]{:S(2)}) collective-permute-start(bf16[16,4096]{1,0:T(8,128)(2,1)} %collective-permute-done.168), channel_id=1, source_target_pairs={{0,1},{1,2},{2,3},{3,0},{4,5},{5,6},{6,7},{7,4},{8,9},{9,10},{10,1... | collective-permute-start | bytes 393224 | tf_op jit(solution)/shard_map/ppermute | solution.py:160
  452.4 119.1 %collective-permute-start.171 = (bf16[16,4096]{1,0:T(8,128)(2,1)}, bf16[16,4096]{1,0:T(8,128)(2,1)}, u32[]{:S(2)}, u32[]{:S(2)}) collective-permute-start(bf16[16,4096]{1,0:T(8,128)(2,1)} %collective-permute-done.168), channel_id=1, source_target_pairs={{0,16},{4,20},{8,24},{12,28},{16,0},{20,4},{24,8},{28,12},{1,17},{... | collective-permute-start | bytes 393224 | tf_op jit(solution)/shard_map/ppermute | solution.py:130
  520.4 64.0 %collective-permute-start.174 = (bf16[16,4096]{1,0:T(8,128)(2,1)}, bf16[16,4096]{1,0:T(8,128)(2,1)S(1)}, u32[]{:S(2)}, u32[]{:S(2)}) collective-permute-start(bf16[16,4096]{1,0:T(8,128)(2,1)} %collective-permute-done.168), channel_id=1, source_target_pairs={{0,8},{4,12},{8,0},{12,4},{16,24},{20,28},{24,16},{28,20},{1,9},{5... | collective-permute-start | bytes 393224 | tf_op jit(solution)/shard_map/ppermute | solution.py:130
  558.9 60.3 %collective-permute-start.217 = (bf16[64,1024]{1,0:T(8,128)(2,1)}, bf16[64,1024]{1,0:T(8,128)(2,1)S(1)}, u32[]{:S(2)}, u32[]{:S(2)}) collective-permute-start(bf16[64,1024]{1,0:T(8,128)(2,1)} %collective-permute-done.216), channel_id=1, source_target_pairs={{0,1},{1,2},{2,3},{3,0},{4,5},{5,6},{6,7},{7,4},{8,9},{9,10},{10,1... | collective-permute-start | bytes 393224 | tf_op jit(solution)/shard_map/ppermute | solution.py:160
  569.7 74.4 %collective-permute-start.219 = (bf16[64,1024]{1,0:T(8,128)(2,1)}, bf16[64,1024]{1,0:T(8,128)(2,1)S(1)}, u32[]{:S(2)}, u32[]{:S(2)}) collective-permute-start(bf16[64,1024]{1,0:T(8,128)(2,1)} %collective-permute-done.216), channel_id=1, source_target_pairs={{0,16},{4,20},{8,24},{12,28},{16,0},{20,4},{24,8},{28,12},{1,17},{... | collective-permute-start | bytes 393224 | tf_op jit(solution)/shard_map/ppermute | solution.py:130
  582.6 70.4 %collective-permute-start.222 = (bf16[64,1024]{1,0:T(8,128)(2,1)}, bf16[64,1024]{1,0:T(8,128)(2,1)S(1)}, u32[]{:S(2)}, u32[]{:S(2)}) collective-permute-start(bf16[64,1024]{1,0:T(8,128)(2,1)} %collective-permute-done.216), channel_id=1, source_target_pairs={{0,8},{4,12},{8,0},{12,4},{16,24},{20,28},{24,16},{28,20},{1,9},{5... | collective-permute-start | bytes 393224 | tf_op jit(solution)/shard_map/ppermute | solution.py:130
  611.5 60.4 %collective-permute-start.228 = (bf16[64,1024]{1,0:T(8,128)(2,1)}, bf16[64,1024]{1,0:T(8,128)(2,1)S(1)}, u32[]{:S(2)}, u32[]{:S(2)}) collective-permute-start(bf16[64,1024]{1,0:T(8,128)(2,1)} %collective-permute-done.216), channel_id=1, source_target_pairs={{0,4},{4,0},{8,12},{12,8},{16,20},{20,16},{24,28},{28,24},{1,5},{5... | collective-permute-start | bytes 393224 | tf_op jit(solution)/shard_map/ppermute | solution.py:136
  851.6 199.2 %collective-permute-start.240 = (bf16[4,2,2,16,3072]{4,3,2,1,0:T(8,128)(2,1)}, bf16[4,2,2,16,3072]{4,3,2,1,0:T(8,128)(2,1)}, u32[]{:S(2)}, u32[]{:S(2)}) collective-permute-start(bf16[4,2,2,16,3072]{4,3,2,1,0:T(8,128)(2,1)} %dynamic-slice_bitcast_fusion.5), channel_id=1, source_target_pairs={{0,4},{4,0},{8,12},{12,8},{16,20},{20,16},{24,28},{28,24},{1,5},{5... | collective-permute-start | bytes 4718600 | tf_op jit(solution)/shard_map/ppermute | solution.py:195
  852.9 201.2 %collective-permute-start.253 = (bf16[4,2,2,16,3072]{4,3,2,1,0:T(8,128)(2,1)}, bf16[4,2,2,16,3072]{4,3,2,1,0:T(8,128)(2,1)}, u32[]{:S(2)}, u32[]{:S(2)}) collective-permute-start(bf16[4,2,2,16,3072]{4,3,2,1,0:T(8,128)(2,1)} %dynamic-slice_bitcast_fusion.4), channel_id=1, source_target_pairs={{0,4},{4,0},{8,12},{12,8},{16,20},{20,16},{24,28},{28,24},{1,5},{5... | collective-permute-start | bytes 4718600 | tf_op jit(solution)/shard_map/ppermute | solution.py:195
  857.1 96.4 %collective-permute-start.292 = (bf16[4,2,2,16,1024]{4,3,2,1,0:T(8,128)(2,1)}, bf16[4,2,2,16,1024]{4,3,2,1,0:T(8,128)(2,1)}, u32[]{:S(2)}, u32[]{:S(2)}) collective-permute-start(bf16[4,2,2,16,1024]{4,3,2,1,0:T(8,128)(2,1)} %dynamic-slice_bitcast_fusion.7), channel_id=1, source_target_pairs={{0,4},{4,0},{8,12},{12,8},{16,20},{20,16},{24,28},{28,24},{1,5},{5... | collective-permute-start | bytes 1572872 | tf_op jit(solution)/shard_map/ppermute | solution.py:195
  875.1 80.3 %collective-permute-start.305 = (bf16[4,2,2,16,1024]{4,3,2,1,0:T(8,128)(2,1)}, bf16[4,2,2,16,1024]{4,3,2,1,0:T(8,128)(2,1)}, u32[]{:S(2)}, u32[]{:S(2)}) collective-permute-start(bf16[4,2,2,16,1024]{4,3,2,1,0:T(8,128)(2,1)} %dynamic-slice_bitcast_fusion.6), channel_id=1, source_target_pairs={{0,4},{4,0},{8,12},{12,8},{16,20},{20,16},{24,28},{28,24},{1,5},{5... | collective-permute-start | bytes 1572872 | tf_op jit(solution)/shard_map/ppermute | solution.py:195
  953.2 103.6 %collective-permute-start.318 = (bf16[4,2,2,16,4096]{4,3,2,1,0:T(8,128)(2,1)}, bf16[4,2,2,16,4096]{4,3,2,1,0:T(8,128)(2,1)}, u32[]{:S(2)}, u32[]{:S(2)}) collective-permute-start(bf16[4,2,2,16,4096]{4,3,2,1,0:T(8,128)(2,1)} %dynamic-slice_bitcast_fusion.3), channel_id=1, source_target_pairs={{0,4},{4,0},{8,12},{12,8},{16,20},{20,16},{24,28},{28,24},{1,5},{5... | collective-permute-start | bytes 6291464 | tf_op jit(solution)/shard_map/ppermute | solution.py:195
  953.6 107.1 %collective-permute-start.331 = (bf16[4,2,2,16,4096]{4,3,2,1,0:T(8,128)(2,1)}, bf16[4,2,2,16,4096]{4,3,2,1,0:T(8,128)(2,1)S(1)}, u32[]{:S(2)}, u32[]{:S(2)}) collective-permute-start(bf16[4,2,2,16,4096]{4,3,2,1,0:T(8,128)(2,1)} %dynamic-slice_bitcast_fusion.2), channel_id=1, source_target_pairs={{0,4},{4,0},{8,12},{12,8},{16,20},{20,16},{24,28},{28,24},{1,5},{5... | collective-permute-start | bytes 6291464 | tf_op jit(solution)/shard_map/ppermute | solution.py:195
  1060.7 112.2 %collective-permute-start.319 = (bf16[4,2,16,4096]{3,2,1,0:T(8,128)(2,1)S(1)}, bf16[4,2,16,4096]{3,2,1,0:T(8,128)(2,1)S(1)}, u32[]{:S(2)}, u32[]{:S(2)}) collective-permute-start(bf16[4,2,16,4096]{3,2,1,0:T(8,128)(2,1)S(1)} %fusion.99), channel_id=1, source_target_pairs={{0,16},{4,20},{8,24},{12,28},{16,0},{20,4},{24,8},{28,12},{1,17},{... | collective-permute-start | bytes 3145736 | tf_op jit(solution)/shard_map/ppermute | solution.py:195
  1062.8 111.8 %collective-permute-start.332 = (bf16[4,2,16,4096]{3,2,1,0:T(8,128)(2,1)S(1)}, bf16[4,2,16,4096]{3,2,1,0:T(8,128)(2,1)S(1)}, u32[]{:S(2)}, u32[]{:S(2)}) collective-permute-start(bf16[4,2,16,4096]{3,2,1,0:T(8,128)(2,1)S(1)} %fusion.100), channel_id=1, source_target_pairs={{0,8},{4,12},{8,0},{12,4},{16,24},{20,28},{24,16},{28,20},{1,9},{5... | collective-permute-start | bytes 3145736 | tf_op jit(solution)/shard_map/ppermute | solution.py:195
  1065.1 111.1 %collective-permute-start.345 = (bf16[4,2,64,1024]{3,2,1,0:T(8,128)(2,1)S(1)}, bf16[4,2,64,1024]{3,2,1,0:T(8,128)(2,1)S(1)}, u32[]{:S(2)}, u32[]{:S(2)}) collective-permute-start(bf16[4,2,64,1024]{3,2,1,0:T(8,128)(2,1)S(1)} %fusion.101), channel_id=1, source_target_pairs={{0,16},{4,20},{8,24},{12,28},{16,0},{20,4},{24,8},{28,12},{1,17},{... | collective-permute-start | bytes 3145736 | tf_op jit(solution)/shard_map/ppermute | solution.py:195
  1074.8 102.1 %collective-permute-start.358 = (bf16[4,2,64,1024]{3,2,1,0:T(8,128)(2,1)S(1)}, bf16[4,2,64,1024]{3,2,1,0:T(8,128)(2,1)S(1)}, u32[]{:S(2)}, u32[]{:S(2)}) collective-permute-start(bf16[4,2,64,1024]{3,2,1,0:T(8,128)(2,1)S(1)} %fusion.102), channel_id=1, source_target_pairs={{0,8},{4,12},{8,0},{12,4},{16,24},{20,28},{24,16},{28,20},{1,9},{5... | collective-permute-start | bytes 3145736 | tf_op jit(solution)/shard_map/ppermute | solution.py:195
  (454 other events, 7253.4 us)
